TPU v7x, 32 devices: a whole 2x2x4 slice. The times are simulated.
32 devices in a mesh: dp: 8 (over z, x), tensor: 4 (over y, core).
Axes of the slice: x: 2, y: 2, z: 4, core: 2. Of those that a mesh axis runs over, the one named last changes fastest.
Arguments:
- attn_out: bfloat16 [4096, 2560], P('dp', 'tensor'), may hold values from -6 to 6
- resid: bfloat16 [4096, 5120], P('dp', 'tensor'), may hold values from -6 to 6
- out_proj: bfloat16 [2560, 5120], P('tensor'), may hold values from -0.125 to 0.125
- heads: bfloat16 [5120, 8], P('tensor'), may hold values from -0.078125 to 0.078125
- gain: bfloat16 [5120], P('tensor'), may hold values from 0.25 to 1.75
- lengths: int32 [64], P('dp'), may hold values from 0 to 63
Outputs:
- uwo: float32 [64], P('dp')
- proj_grad: float32 [5120, 2560], P('dp', 'tensor')
- head_grad: float32 [5120, 8], P('tensor')
- gain_grad: float32 [5120], P('tensor')
Inputs may be any that keep to these rules, and one draw needn't show every extreme that they name: Positions 0 to lengths[n] of response n are scored.
All inputs are finite; a program needn't handle non-finite values.
Results may differ from a plain program's by a relative error of at most 0.0085.
Values may be sent and summed in bfloat16 or wider, within the bound.
A program may use at most 128 MiB of HBM per device.

v0:
```python
import jax
import jax.numpy as jnp
from jax import lax
from jax.sharding import PartitionSpec as P

D = 5120
EPS_NORM = 1e-06
EPS_VAR = 1e-05
PENALTY = 0.5


def per_device(attn_out, resid, out_proj, heads, gain, lengths):
    total_rows = attn_out.shape[0]
    resp_dev = lengths.shape[0]
    seq_len = total_rows // resp_dev
    members = heads.shape[1]
    highest = lax.Precision.HIGHEST
    product = jnp.dot(attn_out, out_proj, preferred_element_type=jnp.float32)
    gain_local = gain.astype(jnp.float32)
    heads_local = heads.astype(jnp.float32)
    hidden = resid.astype(jnp.float32) + lax.psum_scatter(
        product.astype(jnp.bfloat16), "tensor", scatter_dimension=1, tiled=True
    ).astype(jnp.float32)
    squares = lax.psum(jnp.sum(hidden * hidden, axis=1), "tensor")
    rinv = lax.rsqrt(squares / D + EPS_NORM)
    normed = hidden * rinv[:, None] * gain_local[None, :]
    scores = lax.psum(jnp.dot(normed, heads_local, precision=highest), "tensor")
    position = lax.broadcasted_iota(jnp.int32, (resp_dev, seq_len), 1)
    inside = position <= lengths[:, None]
    counts = (lengths + 1).astype(jnp.float32)
    per_resp = scores.reshape(resp_dev, seq_len, members)
    rewards = jnp.sum(jnp.where(inside[:, :, None], per_resp, 0.0), axis=1) / counts[:, None]
    total_resp = resp_dev * lax.axis_size("dp")
    first_sum, second_sum = lax.psum(
        (jnp.sum(rewards, axis=0), jnp.sum(rewards * rewards, axis=0)), "dp"
    )
    center = first_sum / total_resp
    spread = second_sum / total_resp - center * center
    zed = (rewards - center[None, :]) * lax.rsqrt(spread + EPS_VAR)[None, :]
    zmean = jnp.mean(zed, axis=1)
    uwo = zmean - PENALTY * jnp.mean((zed - zmean[:, None]) ** 2, axis=1)
    pairs = rewards.reshape(resp_dev // 2, 2, members)
    weight = jax.nn.sigmoid(pairs[:, 1] - pairs[:, 0])
    dreward = jnp.stack([-weight, weight], axis=1).reshape(resp_dev, members)
    dscore = jnp.where(inside[:, :, None], (dreward / counts[:, None])[:, None, :], 0.0).reshape(
        total_rows, members
    )
    dnormed_local = jnp.dot(dscore, heads_local.T, precision=highest)
    inner = lax.psum(jnp.sum(hidden * gain_local[None, :] * dnormed_local, axis=1), "tensor")
    dhidden = (
        rinv[:, None] * gain_local[None, :] * dnormed_local
        - hidden * (rinv**3 * inner / D)[:, None]
    ).astype(jnp.bfloat16)
    head_term = jnp.dot(normed.T, dscore, precision=highest)
    gain_term = jnp.sum(dnormed_local * hidden * rinv[:, None], axis=0)
    head_grad, gain_grad = lax.psum((head_term, gain_term), "dp")
    term = jnp.einsum(
        "rd,rj->dj",
        lax.all_gather(dhidden, "tensor", axis=1, tiled=True),
        attn_out,
        preferred_element_type=jnp.float32,
    )
    proj_grad = lax.psum_scatter(term, "dp", scatter_dimension=0, tiled=True)
    return (uwo, proj_grad, head_grad, gain_grad)


def solution(mesh):
    return jax.shard_map(
        per_device,
        mesh=mesh,
        in_specs=(
            P("dp", "tensor"),
            P("dp", "tensor"),
            P("tensor", None),
            P("tensor", None),
            P("tensor"),
            P("dp"),
        ),
        out_specs=(P("dp"), P("dp", "tensor"), P("tensor", None), P("tensor")),
        check_vma=False,
    )
```

profile of v0, /device:TPU:0, one launch (start us, length us, event | category | flops | bytes accessed | tf_op | source)
XLA Modules:
  0.0 384.5 jit_solution(8206958620141189595)
XLA Ops:
  7.2 0.0 copy-start
  7.2 0.0 reduce-scatter.3.cloned.1.call-start
  7.2 1.0 copy-done
  8.3 8.8 %convolution_convert_fusion = bf16[512,5120]{1,0:T(8,128)(2,1)} fusion(bf16[512,640]{1,0:T(8,128)(2,1)S(1)} %copy-done, bf16[640,5120]{1,0:T(8,128)(2,1)} %param.8), kind=kOutput, calls=%fused_computation | convolution fusion | flops 3358064640 | bytes 12451840 | tf_op jit(solution)/shard_map/dot_general | solution.py:18
  17.1 0.0 reduce-scatter.3.cloned.1.call-update
  17.1 0.0 copy-start.7
  17.1 0.0 all-gather.2.cloned.1.call-start
  17.2 0.6 copy-done.8
  17.7 0.1 iota_compare_fusion
  17.8 0.6 le.18
  18.4 0.1 div.52
  18.5 0.1 copy.14
  18.6 0.0 copy-done.6
  18.6 52.6 %reduce-scatter.3.cloned.1.call-done = bf16[512,1280]{1,0:T(8,128)(2,1)} async-done(((bf16[512,5120]{1,0:T(8,128)(2,1)}), bf16[512,1280]{1,0:T(8,128)(2,1)}) %reduce-scatter.3.cloned.1.call-update) | async-done | bytes 1310736 | tf_op jit(solution)/shard_map/reduce_scatter | solution.py:21
  71.2 0.0 copy-done.1
  71.2 1.9 multiply_reduce_fusion.2
  73.1 5.8 %psum.49 = f32[512]{0:T(512)S(1)} all-reduce(f32[512]{0:T(512)S(1)} %multiply_reduce_fusion.2), channel_id=1, replica_groups=mesh['dp'=8,'tensor'=4] {'tensor'}, use_global_device_ids=true, to_apply=%region_2.0 | all-reduce | flops 512 | bytes 4096 | tf_op jit(solution)/shard_map/psum | solution.py:24
  78.9 0.0 copy-done.7
  78.9 0.0 copy-done.2
  78.9 0.0 copy-start.3
  78.9 1.7 fusion.1
  80.6 0.1 reshape.69
  80.7 0.0 copy-done.3
  80.7 10.3 %psum.50 = f32[8,64,8]{1,0,2:T(8,128)S(1)} all-reduce(f32[8,64,8]{1,0,2:T(8,128)S(1)} %reshape.69), channel_id=1, replica_groups=mesh['dp'=8,'tensor'=4] {'tensor'}, use_global_device_ids=true, to_apply=%region_3.0 | all-reduce | flops 4096 | bytes 32768 | tf_op jit(solution)/shard_map/psum | solution.py:27
  91.0 0.1 select_reduce_fusion
  91.0 0.1 copy.13
  91.1 0.1 copy_divide_fusion
  91.2 0.1 copy.17
  91.3 0.0 copy-done.5
  91.3 0.7 fusion.13
  92.0 0.7 copy.18
  92.7 0.8 bitcast_select_fusion
  93.5 4.6 %multiply_reduce_fusion = (f32[1280]{0:T(1024)}, f32[512]{0:T(512)}, f32[512,1280]{1,0:T(8,128)}) fusion(bf16[512,1280]{1,0:T(8,128)(2,1)S(1)} %copy-done.2, bf16[512,1280]{1,0:T(8,128)(2,1)S(1)} %copy-done.1, f32[512]{0:T(512)} %copy-done.3, f32[1280]{0:T(1024)S(1)} %convert_element_type.22, f32[512,8]{1,0:T(8,128)S(1)} %bitcast_select_fusion, ...), kind=kOutput, calls=%fused_computation.1 | convolution fusion | flops 68811008 | bytes 5294080 | tf_op jit(solution)/shard_map/dot_general | solution.py:48
  98.2 6.8 %psum.53 = f32[512]{0:T(512)} all-reduce(f32[512]{0:T(512)} %get-tuple-element.5), channel_id=1, replica_groups=mesh['dp'=8,'tensor'=4] {'tensor'}, use_global_device_ids=true, to_apply=%region_12.13 | all-reduce | flops 512 | bytes 4096 | tf_op jit(solution)/shard_map/psum | solution.py:49
  105.0 0.7 fusion.8
  105.7 3.5 subtract_convert_fusion
  109.2 0.0 all-gather.2.cloned.1.call-update
  109.2 0.2 reduce-scatter.5.cloned.1.call-start
  109.5 40.8 %all-gather.2.cloned.1.call-done = bf16[512,5120]{1,0:T(8,128)(2,1)} async-done(((bf16[512,1280]{1,0:T(8,128)(2,1)}), bf16[512,5120]{1,0:T(8,128)(2,1)}) %all-gather.2.cloned.1.call-update) | async-done | bytes 5242896 | tf_op jit(solution)/shard_map/all_gather | solution.py:59
  150.2 11.4 %fusion.16 = f32[5120,640]{1,0:T(8,128)} fusion(bf16[512,5120]{1,0:T(8,128)(2,1)} %all-gather.2.cloned.1.call-done, bf16[512,640]{1,0:T(8,128)(2,1)S(1)} %copy-done), kind=kOutput, calls=%fused_computation.40 | convolution fusion | flops 3355443200 | bytes 19005440 | tf_op jit(solution)/shard_map/rd,rj->dj/dot_general | solution.py:57
  161.7 0.0 reduce-scatter.5.cloned.1.call-update
  161.7 0.7 copy-done.4
  162.3 2.5 fusion
  164.9 41.5 %all-reduce = (f32[8]{0:T(128)S(1)}, f32[8]{0:T(128)S(1)}, f32[1280,8]{0,1:T(8,128)}, f32[1280]{0:T(1024)}) all-reduce(f32[8]{0:T(128)} %get-tuple-element.7, f32[8]{0:T(128)} %get-tuple-element.6, f32[1280,8]{0,1:T(8,128)} %fusion, f32[1280]{0:T(1024)} %get-tuple-element.4), channel_id=1, replica_groups=mesh['dp'=8,'tensor'=4] {'dp'}, use_global_device_ids=true, to_apply=%region_8.9 | all-reduce | flops 11536 | bytes 92288 | tf_op jit(solution)/shard_map/psum | solution.py:34
  206.4 0.8 fusion.6
  207.1 0.8 multiply_reduce_fusion.3
  207.9 0.5 multiply_subtract_fusion
  208.4 169.5 %reduce-scatter.5.cloned.1.call-done = f32[640,640]{1,0:T(8,128)} async-done(((f32[5120,640]{1,0:T(8,128)}), f32[640,640]{1,0:T(8,128)}) %reduce-scatter.5.cloned.1.call-update) | async-done | bytes 1638416 | tf_op jit(solution)/shard_map/reduce_scatter | solution.py:63
  (14 shorter events, 0.1 us)
Async XLA Ops:
  7.2 1.1 copy-start
  7.2 64.0 %reduce-scatter.3.cloned.1.call-start = ((), (), s32[]{:S(2)}) async-start(), calls=%async_computation.2 | async-start | bytes 6553600 | tf_op jit(solution)/shard_map/reduce_scatter | solution.py:21
  17.1 0.7 copy-start.8
  17.1 1.5 copy-start.6
  17.1 54.1 %copy-start.1 = (bf16[512,1280]{1,0:T(8,128)(2,1)S(1)}, bf16[512,1280]{1,0:T(8,128)(2,1)}, u32[]{:S(2)}) copy-start(bf16[512,1280]{1,0:T(8,128)(2,1)} %param.7) | copy-start | bytes 3932164
  17.1 61.8 %copy-start.7 = (bf16[1280,8]{0,1:T(8,128)(2,1)S(1)}, bf16[1280,8]{0,1:T(8,128)(2,1)}, u32[]{:S(2)}) copy-start(bf16[1280,8]{0,1:T(8,128)(2,1)} %param.9) | copy-start | bytes 61444
  17.1 133.1 %all-gather.2.cloned.1.call-start = ((), (), s32[]{:S(2)}) async-start(), calls=%async_computation.3 | async-start | bytes 6553600 | tf_op jit(solution)/shard_map/all_gather | solution.py:59
  18.4 72.9 %copy-start.5 = (f32[8]{0:T(128)}, f32[8]{0:T(128)S(1)}, u32[]{:S(2)}) copy-start(f32[8]{0:T(128)S(1)} %add_convert_fusion) | copy-start | bytes 100
  71.2 7.7 %copy-start.2 = (bf16[512,1280]{1,0:T(8,128)(2,1)S(1)}, bf16[512,1280]{1,0:T(8,128)(2,1)}, u32[]{:S(2)}) copy-start(bf16[512,1280]{1,0:T(8,128)(2,1)} %reduce-scatter.3.cloned.1.call-done) | copy-start | bytes 3932164
  78.9 1.8 copy-start.3
  109.2 268.7 %reduce-scatter.5.cloned.1.call-start = ((), (), s32[]{:S(2)}) async-start(), calls=%async_computation.4 | async-start | bytes 14745600 | tf_op jit(solution)/shard_map/reduce_scatter | solution.py:63
  161.7 0.7 copy-start.4
Sparse Core Ops, SparseCore 0:
  17.2 53.8 reduce-scatter.2
  109.4 40.8 all-gather.1
  161.8 216.0 reduce-scatter.4
where the time goes:
time: 385 us; the launch traced here: 384 us
  waiting for transfers between devices  263 us (68%)
  blocking collectives  64.3 us (17%)
  matrix products  29.2 us (8%)
  between operations  13.8 us (4%)
  other arithmetic  9.97 us (3%)
  local copies, waits for them, and re-layouts  3.95 us (1%)
    reduce_scatter x1, waiting for transfers between devices, per_device(): proj_grad = lax.psum_scatter(term, 'dp', scatter_dimension=0, tiled=True)  170 us
    reduce_scatter x1, waiting for transfers between devices, per_device(): lax.psum_scatter(product.astype(jnp.bfloat16), 'tensor', scatter_dimensio...  52.6 us
    psum x1, blocking collectives, per_device(): lax.psum((jnp.sum(rewards, axis=0), jnp.sum(rewards * rewards, axis=0)),...  41.5 us
    all_gather x1, waiting for transfers between devices, per_device(): lax.all_gather(dhidden, 'tensor', axis=1, tiled=True)  40.8 us
    dot_general x1, matrix products, per_device(): jnp.einsum('rd,rj->dj', lax.all_gather(dhidden, 'tensor', axis=1, tiled=T...  11.4 us
    psum x1, blocking collectives, per_device(): scores = lax.psum(jnp.dot(normed, heads_local, precision=highest), 'tensor')  10.3 us
    dot_general x1, matrix products, per_device(): product = jnp.dot(attn_out, out_proj, preferred_element_type=jnp.float32)  8.81 us
  transfers between devices with their start and end apart: 3, of which 3 were waited for; matrix products, arithmetic and copies ran while one was open for 1% of the time, Pallas kernels for 0%

commit v1 on v0

--- a/solution.py
+++ b/solution.py
@@ -2,6 +2,7 @@
 import jax.numpy as jnp
 from jax import lax
 from jax.sharding import PartitionSpec as P
+from jax.lax import axis_index, axis_size, ppermute
 
 D = 5120
 EPS_NORM = 1e-06
@@ -54,11 +55,34 @@
     head_term = jnp.dot(normed.T, dscore, precision=highest)
     gain_term = jnp.sum(dnormed_local * hidden * rinv[:, None], axis=0)
     head_grad, gain_grad = lax.psum((head_term, gain_term), "dp")
-    term = jnp.einsum(
-        "rd,rj->dj",
-        lax.all_gather(dhidden, "tensor", axis=1, tiled=True),
-        attn_out,
-        preferred_element_type=jnp.float32,
+
+    def floor_meet(view, axis_key, in_dim, page, along_dim):
+        mixed_arr = axis_size(axis_key)
+        seen_now = axis_index(axis_key)
+        after, inter, tall = (mixed_arr, seen_now, view.shape[in_dim])
+        made = []
+        u = 0
+        while u < after:
+            e_now = (
+                ppermute(view, axis_key, [(pp, (pp + 1) % after) for pp in range(after)])
+                if u + 1 < after
+                else view
+            )
+            back = page(view, (inter - u) % after * tall)
+            made.append(back)
+            view = e_now
+            u = u + 1
+        shaped = jnp.concatenate(made[::-1], along_dim)
+        return jnp.roll(shaped, (inter + 1) * made[0].shape[along_dim], along_dim)
+
+    term = floor_meet(
+        dhidden,
+        "tensor",
+        1,
+        lambda own_block, at: jnp.einsum(
+            "rd,rj->dj", own_block, attn_out, preferred_element_type=jnp.float32
+        ),
+        along_dim=0,
     )
     proj_grad = lax.psum_scatter(term, "dp", scatter_dimension=0, tiled=True)
     return (uwo, proj_grad, head_grad, gain_grad)

time: 385 us -> 416 us (1.081)
  local copies, waits for them, and re-layouts: 3.95 us -> 23.8 us
  waiting for transfers between devices: 263 us -> 273 us
    ppermute x0 -> x3, waiting for transfers between devices: none -> 51.5 us  [floor_meet(): ppermute(view, axis_key, [(pp, (pp + 1) % after) for pp in range(after)])]
    all_gather x1 -> x0, waiting for transfers between devices: 40.8 us -> none  [per_device(): lax.all_gather(dhidden, 'tensor', axis=1, tiled=True)]
    dynamic_slice x0 -> x1, local copies, waits for them, and re-layouts: none -> 10.5 us  [floor_meet(): return jnp.roll(shaped, (inter + 1) * made[0].shape[along_dim], along_dim)]
    unnamed x18 -> x29, local copies, waits for them, and re-layouts: 2.29 us -> 9.76 us
    dot_general x1 -> x4, matrix products: 11.4 us -> 14.5 us  [per_device(): jnp.einsum('rd,rj->dj', own_block, attn_out, preferred_element_type=jnp.f...]
  transfers between devices with their start and end apart: 3 -> 5, of which waited for: 3 -> 5; matrix products, arithmetic and copies ran while one was open for 1% -> 1% of each run, Pallas kernels for 0% -> 0%
where the time goes in v1:
time: 416 us
  waiting for transfers between devices  273 us (66%)
  blocking collectives  64 us (15%)
  matrix products  32.1 us (8%)
  local copies, waits for them, and re-layouts  23.8 us (6%)
  between operations  14.2 us (3%)
  other arithmetic  8.57 us (2%)
    reduce_scatter x1, waiting for transfers between devices, per_device(): proj_grad = lax.psum_scatter(term, 'dp', scatter_dimension=0, tiled=True)  169 us
    reduce_scatter x1, waiting for transfers between devices, per_device(): lax.psum_scatter(product.astype(jnp.bfloat16), 'tensor', scatter_dimensio...  52.5 us
    ppermute x3, waiting for transfers between devices, floor_meet(): ppermute(view, axis_key, [(pp, (pp + 1) % after) for pp in range(after)])  51.5 us
    psum x1, blocking collectives, per_device(): lax.psum((jnp.sum(rewards, axis=0), jnp.sum(rewards * rewards, axis=0)),...  41.7 us
    dot_general x4, matrix products, per_device(): jnp.einsum('rd,rj->dj', own_block, attn_out, preferred_element_type=jnp.f...  14.5 us
    dynamic_slice x1, local copies, waits for them, and re-layouts, floor_meet(): return jnp.roll(shaped, (inter + 1) * made[0].shape[along_dim], along_dim)  10.5 us
    psum x1, blocking collectives, per_device(): scores = lax.psum(jnp.dot(normed, heads_local, precision=highest), 'tensor')  10.3 us
    unnamed x29, local copies, waits for them, and re-layouts  9.76 us
  transfers between devices with their start and end apart: 5, of which 5 were waited for; matrix products, arithmetic and copies ran while one was open for 1% of the time, Pallas kernels for 0%

profile of v1, /device:TPU:0, one launch (start us, length us, event | category | flops | bytes accessed | tf_op | source)
XLA Modules:
  0.0 415.6 jit_solution(12625820814611946100)
XLA Ops:
  7.2 0.0 reduce-scatter.3.cloned.1.call-start
  7.2 1.0 copy-done
  8.3 8.8 %convolution_convert_fusion = bf16[512,5120]{1,0:T(8,128)(2,1)} fusion(bf16[512,640]{1,0:T(8,128)(2,1)S(1)} %copy-done, bf16[640,5120]{1,0:T(8,128)(2,1)} %param.8), kind=kOutput, calls=%fused_computation | convolution fusion | flops 3358064640 | bytes 12451840 | tf_op jit(solution)/shard_map/dot_general | solution.py:19
  17.1 0.0 reduce-scatter.3.cloned.1.call-update
  17.1 0.0 reduce-scatter.5.cloned.1.call-start
  17.2 0.6 copy-done.10
  17.8 0.1 div.52
  17.9 0.1 copy.14
  18.0 0.1 iota_compare_fusion
  18.0 0.6 le.18
  18.6 52.5 %reduce-scatter.3.cloned.1.call-done = bf16[512,1280]{1,0:T(8,128)(2,1)} async-done(((bf16[512,5120]{1,0:T(8,128)(2,1)}), bf16[512,1280]{1,0:T(8,128)(2,1)}) %reduce-scatter.3.cloned.1.call-update) | async-done | bytes 1310736 | tf_op jit(solution)/shard_map/reduce_scatter | solution.py:22
  71.2 1.9 multiply_reduce_fusion.2
  73.1 5.8 %psum.49 = f32[512]{0:T(512)S(1)} all-reduce(f32[512]{0:T(512)S(1)} %multiply_reduce_fusion.2), channel_id=1, replica_groups=mesh['dp'=8,'tensor'=4] {'tensor'}, use_global_device_ids=true, to_apply=%region_2.0 | all-reduce | flops 512 | bytes 4096 | tf_op jit(solution)/shard_map/psum | solution.py:25
  78.9 1.7 fusion.1
  80.6 0.1 reshape.69
  80.7 10.3 %psum.50 = f32[8,64,8]{1,0,2:T(8,128)S(1)} all-reduce(f32[8,64,8]{1,0,2:T(8,128)S(1)} %reshape.69), channel_id=1, replica_groups=mesh['dp'=8,'tensor'=4] {'tensor'}, use_global_device_ids=true, to_apply=%region_3.0 | all-reduce | flops 4096 | bytes 32768 | tf_op jit(solution)/shard_map/psum | solution.py:28
  91.0 0.1 select_reduce_fusion
  91.0 0.1 copy.13
  91.1 0.1 copy_divide_fusion
  91.2 0.1 copy.17
  91.3 0.7 fusion.13
  92.0 0.7 copy.18
  92.7 0.8 bitcast_select_fusion
  93.5 4.6 %multiply_reduce_fusion = (f32[1280]{0:T(1024)}, f32[512]{0:T(512)}, f32[512,1280]{1,0:T(8,128)}) fusion(bf16[512,1280]{1,0:T(8,128)(2,1)S(1)} %copy-done.3, bf16[512,1280]{1,0:T(8,128)(2,1)S(1)} %copy-done.2, f32[512]{0:T(512)} %copy-done.7, f32[1280]{0:T(1024)S(1)} %convert_element_type.22, f32[512,8]{1,0:T(8,128)S(1)} %bitcast_select_fusion, ...), kind=kOutput, calls=%fused_computation.1 | convolution fusion | flops 68811008 | bytes 5294080 | tf_op jit(solution)/shard_map/dot_general | solution.py:49
  98.1 6.3 %psum.53 = f32[512]{0:T(512)S(1)} all-reduce(f32[512]{0:T(512)} %get-tuple-element.5), channel_id=1, replica_groups=mesh['dp'=8,'tensor'=4] {'tensor'}, use_global_device_ids=true, to_apply=%region_12.13 | all-reduce | flops 512 | bytes 4096 | tf_op jit(solution)/shard_map/psum | solution.py:50
  104.4 2.8 subtract_convert_fusion
  107.2 0.1 collective-permute-start
  107.3 17.0 %collective-permute-done = bf16[512,1280]{1,0:T(8,128)(2,1)S(1)} collective-permute-done((bf16[512,1280]{1,0:T(8,128)(2,1)S(1)}, bf16[512,1280]{1,0:T(8,128)(2,1)S(1)}, u32[]{:S(2)}, u32[]{:S(2)}) %collective-permute-start) | collective-permute-done | bytes 1310752 | tf_op jit(solution)/shard_map/ppermute | solution.py:67
  124.3 1.1 copy-done.5
  125.3 17.1 %collective-permute-done.1 = bf16[512,1280]{1,0:T(8,128)(2,1)} collective-permute-done((bf16[512,1280]{1,0:T(8,128)(2,1)S(1)}, bf16[512,1280]{1,0:T(8,128)(2,1)}, u32[]{:S(2)}, u32[]{:S(2)}) %collective-permute-start.1) | collective-permute-done | bytes 1310752 | tf_op jit(solution)/shard_map/ppermute | solution.py:67
  142.5 17.3 %collective-permute-done.2 = bf16[512,1280]{1,0:T(8,128)(2,1)} collective-permute-done((bf16[512,1280]{1,0:T(8,128)(2,1)}, bf16[512,1280]{1,0:T(8,128)(2,1)}, u32[]{:S(2)}, u32[]{:S(2)}) %collective-permute-start.2) | collective-permute-done | bytes 1310752 | tf_op jit(solution)/shard_map/ppermute | solution.py:67
  159.8 4.2 %constant_dynamic-update-slice_fusion.7 = (f32[10240,640]{1,0:T(8,128)}, f32[1280,640]{1,0:T(8,128)S(1)}) fusion(bf16[512,1280]{1,0:T(8,128)(2,1)} %collective-permute-done.2, bf16[512,640]{1,0:T(8,128)(2,1)S(1)} %copy-done), kind=kOutput, calls=%fused_computation.22 | convolution fusion | flops 838860800 | bytes 8519680 | tf_op jit(solution)/shard_map/rd,rj->dj/dot_general | solution.py:82
  164.0 4.4 %constant_dynamic-update-slice_fusion.6 = (f32[10240,640]{1,0:T(8,128)}, f32[1280,640]{1,0:T(8,128)S(1)}) fusion(f32[10240,640]{1,0:T(8,128)} %get-tuple-element.18, bf16[512,1280]{1,0:T(8,128)(2,1)} %collective-permute-done.1, bf16[512,640]{1,0:T(8,128)(2,1)S(1)} %copy-done), kind=kOutput, calls=%fused_computation.21 | convolution fusion | flops 838860800 | bytes 8519680 | tf_op jit(solution)/shard_map/rd,rj->dj/dot_general | solution.py:82
  168.4 3.0 constant_dynamic-update-slice_fusion.5
  171.4 2.9 constant_dynamic-update-slice_fusion.4
  174.3 1.9 constant_dynamic-update-slice_fusion.3
  176.2 1.9 constant_dynamic-update-slice_fusion.2
  178.1 2.0 constant_dynamic-update-slice_fusion.1
  180.0 1.9 constant_dynamic-update-slice_fusion
  182.0 10.5 %constant_dynamic-slice_fusion = f32[5120,640]{1,0:T(8,128)} fusion(f32[10240,640]{1,0:T(8,128)} %constant_dynamic-update-slice_fusion, s32[]{:T(128)S(6)} %select_n.25), kind=kLoop, calls=%fused_computation.44 | loop fusion | bytes 26214404 | tf_op jit(solution)/shard_map/jit(_roll_dynamic)/dynamic_slice | solution.py:76
  192.5 0.0 reduce-scatter.5.cloned.1.call-update
  192.5 1.3 copy-done.4
  193.8 2.5 fusion
  196.3 41.7 %all-reduce = (f32[8]{0:T(128)S(1)}, f32[8]{0:T(128)S(1)}, f32[1280,8]{0,1:T(8,128)}, f32[1280]{0:T(1024)}) all-reduce(f32[8]{0:T(128)} %get-tuple-element.7, f32[8]{0:T(128)} %get-tuple-element.6, f32[1280,8]{0,1:T(8,128)} %fusion, f32[1280]{0:T(1024)} %get-tuple-element.4), channel_id=1, replica_groups=mesh['dp'=8,'tensor'=4] {'dp'}, use_global_device_ids=true, to_apply=%region_8.9 | all-reduce | flops 11536 | bytes 92288 | tf_op jit(solution)/shard_map/psum | solution.py:35
  238.0 0.7 fusion.6
  238.7 0.7 multiply_reduce_fusion.3
  239.5 0.5 multiply_subtract_fusion
  240.0 168.7 %reduce-scatter.5.cloned.1.call-done = f32[640,640]{1,0:T(8,128)} async-done(((f32[5120,640]{1,0:T(8,128)}), f32[640,640]{1,0:T(8,128)}) %reduce-scatter.5.cloned.1.call-update) | async-done | bytes 1638416 | tf_op jit(solution)/shard_map/reduce_scatter | solution.py:87
  (33 shorter events, 0.1 us)
Async XLA Ops:
  7.2 1.1 copy-start
  7.2 64.0 %reduce-scatter.3.cloned.1.call-start = ((), (), s32[]{:S(2)}) async-start(), calls=%async_computation.2 | async-start | bytes 6553600 | tf_op jit(solution)/shard_map/reduce_scatter | solution.py:22
  17.1 0.7 copy-start.10
  17.1 0.7 copy-start.12
  17.1 54.1 %copy-start.2 = (bf16[512,1280]{1,0:T(8,128)(2,1)S(1)}, bf16[512,1280]{1,0:T(8,128)(2,1)}, u32[]{:S(2)}) copy-start(bf16[512,1280]{1,0:T(8,128)(2,1)} %param.7) | copy-start | bytes 3932164
  17.1 61.8 %copy-start.11 = (bf16[1280,8]{0,1:T(8,128)(2,1)S(1)}, bf16[1280,8]{0,1:T(8,128)(2,1)}, u32[]{:S(2)}) copy-start(bf16[1280,8]{0,1:T(8,128)(2,1)} %param.9) | copy-start | bytes 61444
  17.1 391.6 %reduce-scatter.5.cloned.1.call-start = ((), (), s32[]{:S(2)}) async-start(), calls=%async_computation.3 | async-start | bytes 14745600 | tf_op jit(solution)/shard_map/reduce_scatter | solution.py:87
  17.8 73.5 %copy-start.9 = (f32[8]{0:T(128)}, f32[8]{0:T(128)S(1)}, u32[]{:S(2)}) copy-start(f32[8]{0:T(128)S(1)} %add_convert_fusion) | copy-start | bytes 100
  71.2 7.7 %copy-start.3 = (bf16[512,1280]{1,0:T(8,128)(2,1)S(1)}, bf16[512,1280]{1,0:T(8,128)(2,1)}, u32[]{:S(2)}) copy-start(bf16[512,1280]{1,0:T(8,128)(2,1)} %reduce-scatter.3.cloned.1.call-done) | copy-start | bytes 3932164
  78.9 1.8 copy-start.7
  107.2 17.1 %collective-permute-start = (bf16[512,1280]{1,0:T(8,128)(2,1)S(1)}, bf16[512,1280]{1,0:T(8,128)(2,1)S(1)}, u32[]{:S(2)}, u32[]{:S(2)}) collective-permute-start(bf16[512,1280]{1,0:T(8,128)(2,1)S(1)} %subtract_convert_fusion), channel_id=1, source_target_pairs={{0,1},{1,2},{2,3},{3,0},{4,5},{5,6},{6,7},{7,4},{8,9},{9,10},{10,1... | collective-permute-start | bytes 3932168 | tf_op jit(solution)/shard_map/ppermute | solution.py:67
  124.3 1.1 copy-start.5
  125.3 17.1 %collective-permute-start.1 = (bf16[512,1280]{1,0:T(8,128)(2,1)S(1)}, bf16[512,1280]{1,0:T(8,128)(2,1)}, u32[]{:S(2)}, u32[]{:S(2)}) collective-permute-start(bf16[512,1280]{1,0:T(8,128)(2,1)S(1)} %collective-permute-done), channel_id=1, source_target_pairs={{0,1},{1,2},{2,3},{3,0},{4,5},{5,6},{6,7},{7,4},{8,9},{9,10},{10,1... | collective-permute-start | bytes 3932168 | tf_op jit(solution)/shard_map/ppermute | solution.py:67
  142.5 17.3 %collective-permute-start.2 = (bf16[512,1280]{1,0:T(8,128)(2,1)}, bf16[512,1280]{1,0:T(8,128)(2,1)}, u32[]{:S(2)}, u32[]{:S(2)}) collective-permute-start(bf16[512,1280]{1,0:T(8,128)(2,1)} %collective-permute-done.1), channel_id=1, source_target_pairs={{0,1},{1,2},{2,3},{3,0},{4,5},{5,6},{6,7},{7,4},{8,9},{9,10},{10,1... | collective-permute-start | bytes 3932168 | tf_op jit(solution)/shard_map/ppermute | solution.py:67
  164.0 4.4 %copy-start.6 = (bf16[512,1280]{1,0:T(8,128)(2,1)S(1)}, bf16[512,1280]{1,0:T(8,128)(2,1)}, u32[]{:S(2)}) copy-start(bf16[512,1280]{1,0:T(8,128)(2,1)} %copy-done.5) | copy-start | bytes 3932164
  192.5 1.3 copy-start.4
  192.5 1.3 copy-start.8
  193.8 215.0 %copy-start.1 = (bf16[512,640]{1,0:T(8,128)(2,1)S(1)}, bf16[512,640]{1,0:T(8,128)(2,1)}, u32[]{:S(2)}) copy-start(bf16[512,640]{1,0:T(8,128)(2,1)} %param.6) | copy-start | bytes 1966084
Sparse Core Ops, SparseCore 0:
  17.2 53.8 reduce-scatter.2
  192.6 216.0 reduce-scatter.4
